TPU v7x, 32 devices: a whole 2x2x4 slice. The times are simulated.
32 devices in a mesh: groups: 2 (over x), ctx: 16 (over z, y, core).
Axes of the slice: x: 2, y: 2, z: 4, core: 2. Of those that a mesh axis runs over, the one named last changes fastest.
Arguments:
- hidden_in: bfloat16 [4096, 2048], P(('groups', 'ctx')), parts along dimension 0, may hold values from -6 to 6
- span_order: int32 [32, 2], P('groups'), parts along dimension 0, may hold values from 0 to 31, as said below
- norm_gain: float32 [2048], replicated, may hold values from 0.5 to 1.5
- w_query: bfloat16 [2048, 2048], replicated, may hold values from -0.125 to 0.125
- w_key: bfloat16 [2048, 256], replicated, may hold values from -0.125 to 0.125
- w_value: bfloat16 [2048, 256], replicated, may hold values from -0.125 to 0.125
- query_gain: float32 [128], replicated, may hold values from 1.5 to 7
- key_gain: float32 [128], replicated, may hold values from 1.5 to 7
Outputs:
- attended: bfloat16 [4096, 2048], P(('groups', 'ctx')), parts along dimension 0
There are 2 independent parts, one for each index of `groups`. A program takes and returns all parts, laid end to end along the dimension named above; an argument that names none is the same for every part. Nothing has to cross between parts.
Inputs may be any that keep to these rules, and one draw needn't show every extreme that they name: `span_order`: row d holds a span c and the span 2 * 16 - 1 - c with c < 16; the rows together name every span once; a device's first 64 rows are its column 0 span.
All inputs are finite; a program needn't handle non-finite values.
Results may differ from a plain program's by a relative error of at most 0.0075.
The roundings to bfloat16 on the way count: a program that leaves them out, or rounds other values in their place, can miss the bound.
Values may be sent and summed in bfloat16 or wider, within the bound.
A program may use at most 128 MiB of HBM per device.

v0:
```python
import jax
import jax.numpy as jnp
from jax import lax
from jax.sharding import PartitionSpec as P

HEADS = 16
KV_HEADS = 2
HEAD = 128


EPSILON = 1e-06
THETA = 1000000.0


def partner(x, axis, bit):
    return lax.ppermute(x, axis, [(i, i ^ 1 << bit) for i in range(lax.axis_size(axis))])


def scaled(entries, gains):
    mean_square = jnp.mean(entries * entries, axis=-1, keepdims=True)
    return entries * lax.rsqrt(mean_square + EPSILON) * gains


def rotated(entries, position):
    head_width = entries.shape[-1]
    halfway = head_width // 2
    exponent = jnp.arange(halfway, dtype=jnp.float32) * (2.0 / head_width)
    inverse = jnp.power(jnp.float32(THETA), -exponent)
    angles = position.astype(jnp.float32)[:, None] * inverse[None, :]
    cosine = jnp.cos(angles)[:, None, :]
    sine_part = jnp.sin(angles)[:, None, :]
    first_half = entries[..., :halfway]
    second = entries[..., halfway:]
    return jnp.concatenate(
        [first_half * cosine - second * sine_part, second * cosine + first_half * sine_part],
        axis=-1,
    )


def project(hidden_in, norm_gain, w_query, w_key, w_value, query_gain, key_gain, position):
    row_count = hidden_in.shape[0]
    normed = scaled(hidden_in.astype(jnp.float32), norm_gain).astype(jnp.bfloat16)
    queries = jnp.dot(normed, w_query, preferred_element_type=jnp.float32).reshape(
        row_count, HEADS, HEAD
    )
    queries = rotated(scaled(queries, query_gain), position).astype(jnp.bfloat16)
    key_heads = jnp.dot(normed, w_key, preferred_element_type=jnp.float32).reshape(
        row_count, KV_HEADS, HEAD
    )
    key_heads = rotated(scaled(key_heads, key_gain), position).astype(jnp.bfloat16)
    values = jnp.dot(normed, w_value, preferred_element_type=jnp.float32).astype(jnp.bfloat16)
    return (queries, key_heads, values)


def update(carried, rows_query, rows_position, block_keys, block_values, block_position):
    keys_three = block_keys.reshape(-1, KV_HEADS, HEAD)
    values_three = block_values.reshape(-1, KV_HEADS, HEAD)
    scores = jnp.einsum(
        "ncd,crd->cnr", keys_three, rows_query, preferred_element_type=jnp.float32
    ) * HEAD ** (-0.5)
    visible = (block_position[:, None] <= rows_position[None, :])[None]
    scores = jnp.where(visible, scores, -1e30)
    row_peak, row_total, row_accum = carried
    new_peak = jnp.maximum(row_peak, jnp.max(scores, axis=1))
    decay = jnp.exp(row_peak - new_peak)
    weight = jnp.where(visible, jnp.exp(scores - new_peak[:, None, :]), 0.0)
    row_total = row_total * decay + jnp.sum(weight, axis=1)
    product = jnp.einsum(
        "cnr,ncd->crd",
        weight.astype(jnp.bfloat16),
        values_three,
        preferred_element_type=jnp.float32,
    )
    row_accum = row_accum * decay[..., None] + product
    return (new_peak, row_total, row_accum)


def body(hidden_in, span_order, norm_gain, w_query, w_key, w_value, query_gain, key_gain):
    tok_rows = hidden_in.shape[0]
    half_rows = tok_rows // 2
    group_size = HEADS // KV_HEADS
    devices = lax.axis_size("ctx")
    own_index = lax.axis_index("ctx")
    device_ids = jnp.arange(devices, dtype=jnp.int32)
    within = jnp.arange(tok_rows, dtype=jnp.int32)

    def locate(spans):
        early_place = spans[..., 0:1] * half_rows + within
        late_place = spans[..., 1:2] * half_rows + within - half_rows
        return jnp.where(within < half_rows, early_place, late_place)

    own_spans = jnp.sum(jnp.where((device_ids == own_index)[:, None], span_order, 0), axis=0)
    position = locate(own_spans)
    queries, key_heads, values = project(
        hidden_in, norm_gain, w_query, w_key, w_value, query_gain, key_gain, position
    )
    key_flat = key_heads.reshape(tok_rows, KV_HEADS * HEAD)

    def arrange(portion):
        grouped = portion.reshape(half_rows, KV_HEADS, group_size, HEAD)
        return jnp.transpose(grouped, (1, 2, 0, 3)).reshape(KV_HEADS, group_size * half_rows, HEAD)

    early_query = arrange(queries[:half_rows])
    late_query = arrange(queries[half_rows:])
    early_position = jnp.tile(position[:half_rows], group_size)
    late_position = jnp.tile(position[half_rows:], group_size)
    early_limit = jnp.max(position[:half_rows])

    def empty_state():
        return (
            jnp.full((KV_HEADS, group_size * half_rows), -1e30, jnp.float32),
            jnp.zeros((KV_HEADS, group_size * half_rows), jnp.float32),
            jnp.zeros((KV_HEADS, group_size * half_rows, HEAD), jnp.float32),
        )

    initial = (empty_state(), empty_state())

    def absorb(carried, fragment, first_row):
        fragment_keys, fragment_values = fragment
        shards = fragment_keys.shape[0] // tok_rows
        sources = first_row // tok_rows + jnp.arange(shards, dtype=jnp.int32)
        matches = (sources[:, None] == device_ids[None, :])[:, :, None]
        spans = jnp.sum(jnp.where(matches, span_order[None], 0), axis=1)
        key_position = locate(spans)
        grouping = 4 if shards % 4 == 0 else 1
        rounds = shards // grouping
        keys_grouped = fragment_keys.reshape(rounds, grouping, tok_rows, KV_HEADS * HEAD)
        values_grouped = fragment_values.reshape(rounds, grouping, tok_rows, KV_HEADS * HEAD)
        position_grouped = key_position.reshape(rounds, grouping, tok_rows)

        def advance(state_pair, blocks):
            block_keys, block_values, block_position = blocks
            early_state, late_state = state_pair
            late_state = update(
                late_state,
                late_query,
                late_position,
                block_keys.reshape(-1, KV_HEADS * HEAD),
                block_values.reshape(-1, KV_HEADS * HEAD),
                block_position.reshape(-1),
            )
            early_keys = block_keys[:, :half_rows].reshape(-1, KV_HEADS * HEAD)
            early_values = block_values[:, :half_rows].reshape(-1, KV_HEADS * HEAD)
            early_keypos = block_position[:, :half_rows].reshape(-1)
            active = jnp.min(early_keypos) <= early_limit

            def compute_early(inner):
                return update(
                    inner, early_query, early_position, early_keys, early_values, early_keypos
                )

            def keep_early(inner):
                return inner

            early_state = lax.cond(active, compute_early, keep_early, early_state)
            return ((early_state, late_state), None)

        carried, unused = lax.scan(
            advance, carried, (keys_grouped, values_grouped, position_grouped)
        )
        return carried

    final_state = absorb(initial, (key_flat, values), own_index * tok_rows)
    holding = jnp.stack([key_flat, values])
    levels = devices.bit_length() - 1
    for degree in range(levels):
        stride_len = 1 << degree
        received = partner(holding, "ctx", degree)
        partner_first = jnp.bitwise_xor(own_index // stride_len, 1) * stride_len
        final_state = absorb(final_state, (received[0], received[1]), partner_first * tok_rows)
        if degree + 1 < levels:
            upper_half = own_index // stride_len % 2 == 1
            holding = jnp.where(
                upper_half,
                jnp.concatenate([received, holding], axis=1),
                jnp.concatenate([holding, received], axis=1),
            )

    def finish(carried):
        row_peak, row_total, row_accum = carried
        blended = row_accum / row_total[..., None]
        blended = blended.reshape(KV_HEADS, group_size, half_rows, HEAD)
        return jnp.transpose(blended, (2, 0, 1, 3)).reshape(half_rows, HEADS * HEAD)

    early_state, late_state = final_state
    return jnp.concatenate([finish(early_state), finish(late_state)], axis=0).astype(jnp.bfloat16)


def solution(mesh):
    in_specs = (P(("groups", "ctx"), None), P("groups", None), P(), P(), P(), P(), P(), P())
    out_specs = P(("groups", "ctx"), None)
    return jax.shard_map(body, mesh=mesh, in_specs=in_specs, out_specs=out_specs, check_vma=False)
```

profile of v0, /device:TPU:7, one launch (start us, length us, event | category | flops | bytes accessed | tf_op | source)
XLA Modules:
  0.0 162.8 jit_solution(15068756636822303569)
XLA Ops:
  0.1 0.9 select_reduce_fusion.3
  3.0 1.3 fusion.88
  4.4 1.4 fusion.128
  12.7 1.3 fusion.144
  14.0 1.2 fusion.145
  16.5 1.2 fusion.146
  18.9 1.2 fusion.147
  21.3 4.7 %convolution_bitcast_fusion = f32[16,8,16,128]{3,1,2,0:T(8,128)S(1)} fusion(bf16[2048,2048]{1,0:T(8,128)(2,1)} %param.25, bf16[128,2048]{1,0:T(8,128)(2,1)S(1)} %copy-done.7, f32[2048]{0:T(1024)S(1)} %copy-done.21, f32[128]{0:T(128)S(1)} %add_rsqrt_fusion.2), kind=kOutput, calls=%fused_computation.127 | convolution fusion | flops 1074790400 | bytes 9970176 | tf_op jit(solution)/shard_map/dot_general | solution.py:43
  29.6 0.9 broadcast_compare_fusion.7
  31.7 1.3 tile.4
  32.9 1.7 %conditional.5 = ((f32[2,512]{1,0:T(2,128)S(1)}, f32[2,512]{1,0:T(2,128)S(1)}, f32[2,512,128]{2,1,0:T(8,128)S(1)})) conditional(s32[]{:T(128)} %convert_element_type.87, (f32[2,512]{1,0:T(2,128)S(1)}, f32[2,512]{1,0:T(2,128)S(1)}, f32[2,512,128]{2,1,0:T(8,128)S(1)}) %tuple.53, (s32[1,64]{1,0:T(1,128)S(1)}, s32[8,64]{1,0:T(8,128)}, ...), branch_computations={%region_11.12_spmd, %region_12.15_spmd} | conditional | flops 34441216 | bytes 2496800 | solution.py:155
  34.6 1.3 broadcast_select_fusion
  39.7 5.8 %collective-permute-done.1 = bf16[2,256,256]{2,1,0:T(8,128)(2,1)} collective-permute-done((bf16[2,256,256]{2,1,0:T(8,128)(2,1)}, bf16[2,256,256]{2,1,0:T(8,128)(2,1)}, u32[]{:S(2)}, u32[]{:S(2)}) %collective-permute-start.1) | collective-permute-done | bytes 262176 | tf_op jit(solution)/shard_map/ppermute | solution.py:16
  45.5 2.1 %maximum_select_fusion.1 = bf16[2,512,256]{2,1,0:T(8,128)(2,1)} fusion(bf16[2,256,256]{2,1,0:T(8,128)(2,1)} %maximum_select_fusion.2, bf16[2,256,256]{2,1,0:T(8,128)(2,1)} %collective-permute-done.1, pred[]{:T(512)S(6)} %eq.115), kind=kLoop, calls=%fused_computation.153 | loop fusion | flops 2359296 | bytes 1048577 | tf_op jit(solution)/shard_map/jit(_where)/select_n | solution.py:173
  47.6 1.3 collective-permute-start.2
  48.9 1.0 fusion.142
  49.9 11.3 %while.6 = (s32[]{:T(128)}, f32[2,512]{1,0:T(2,128)S(1)}, f32[2,512]{1,0:T(2,128)S(1)}, f32[2,512,128]{2,1,0:T(8,128)S(1)}, f32[2,512]{1,0:T(2,128)S(1)}, /*inde...) while((s32[]{:T(128)}, f32[2,512]{1,0:T(2,128)S(1)}, ...), condition=%wide.region_32.33_spmd.clone, body=%wide.region_24.32_spmd.clone.sunk | while | flops 103059520 | bytes 6770223 | solution.py:158
  57.5 2.0 %conditional.12 = ((f32[2,512]{1,0:T(2,128)S(1)}, f32[2,512]{1,0:T(2,128)S(1)}, f32[2,512,128]{2,1,0:T(8,128)S(1)})) conditional(s32[]{:T(128)} %convert_element_type.144, (f32[2,512]{1,0:T(2,128)S(1)}, f32[2,512]{1,0:T(2,128)S(1)}, f32[2,512,128]{2,1,0:T(8,128)S(1)}) %tuple.170, (s32[1,64]{1,0:T(1,128)S(1)}, s32[64]{0:T(128)}, ...), branch_computations={%region_26.26_spmd, %region_27.29_spmd} | conditional | flops 34441216 | bytes 2892320 | solution.py:155
  61.3 1.1 fusion.141
  63.9 2.8 %maximum_select_fusion = bf16[2,1024,256]{2,1,0:T(8,128)(2,1)} fusion(bf16[2,512,256]{2,1,0:T(8,128)(2,1)} %maximum_select_fusion.1, bf16[2,512,256]{2,1,0:T(8,128)(2,1)} %collective-permute-done.2, pred[]{:T(512)S(6)} %eq.119), kind=kLoop, calls=%fused_computation.142 | loop fusion | flops 4718592 | bytes 2097153 | tf_op jit(solution)/shard_map/jit(_where)/select_n | solution.py:173
  66.7 4.3 %collective-permute-start.3 = (bf16[2,1024,256]{2,1,0:T(8,128)(2,1)}, bf16[2,1024,256]{2,1,0:T(8,128)(2,1)}, u32[]{:S(2)}, u32[]{:S(2)}) collective-permute-start(bf16[2,1024,256]{2,1,0:T(8,128)(2,1)} %maximum_select_fusion), channel_id=1, source_target_pairs={{0,8},{1,9},{2,10},{3,11},{4,12},{5,13},{6,14},{7,15},{8,0},{9,1},... | collective-permute-start | bytes 3145736 | tf_op jit(solution)/shard_map/ppermute | solution.py:16
  71.0 1.9 %fusion.82 = (f32[2,512]{1,0:T(2,128)S(1)}, f32[2,512,512]{2,1,0:T(8,128)}) fusion(pred[512,512]{1,0:T(8,128)(4,1)S(1)} %copy-done.9, bf16[2,512,128]{2,1,0:T(8,128)(2,1)S(1)} %get-tuple-element.1263, bf16[512,2,128]{2,1,0:T(2,128)(2,1)S(1)} %copy-done.15), kind=kOutput, calls=%fused_computation.124 | convolution fusion | flops 135789568 | bytes 2887680 | tf_op jit(solution)/shard_map/while/body/eval_jaxpr/ncd,crd->cnr/dot_general | solution.py:58
  73.2 2.3 %fusion.84 = f32[2,512]{1,0:T(2,128)S(1)} fusion(f32[2,512,512]{2,1,0:T(8,128)} %get-tuple-element.889, f32[2,512]{1,0:T(2,128)S(1)} %max.57, pred[512,512]{1,0:T(8,128)(4,1)} %broadcast_compare_fusion.7), kind=kLoop, calls=%fused_computation.126 | loop fusion | flops 2620416 | bytes 2367488 | tf_op jit(solution)/shard_map/while/body/eval_jaxpr/reduce_sum | solution.py:67
  76.1 2.7 %convolution_add_fusion.7 = f32[2,512,128]{2,1,0:T(8,128)} fusion(f32[2,512,512]{2,1,0:T(8,128)S(1)} %copy-done.8, f32[2,512]{1,0:T(2,128)S(1)} %max.57, pred[512,512]{1,0:T(8,128)(4,1)S(1)} %copy-done.10, f32[2,512,128]{2,1,0:T(8,128)S(1)} %get-tuple-element.493, bf16[512,2,128]{2,1,0:T(2,128)(2,1)} %reshape.957, f32[2,512]{1,0:T(2,128)S(1)} %get-tuple-element.811), kind=kOutput, calls=%fused_computation.130 | convolution fusion | flops 137101312 | bytes 3678208 | tf_op jit(solution)/shard_map/while/body/eval_jaxpr/cnr,ncd->crd/dot_general | solution.py:68
  78.8 38.1 %collective-permute-done.3 = bf16[2,1024,256]{2,1,0:T(8,128)(2,1)} collective-permute-done((bf16[2,1024,256]{2,1,0:T(8,128)(2,1)}, bf16[2,1024,256]{2,1,0:T(8,128)(2,1)}, u32[]{:S(2)}, u32[]{:S(2)}) %collective-permute-start.3) | collective-permute-done | bytes 1048608 | tf_op jit(solution)/shard_map/ppermute | solution.py:16
  117.0 2.1 %fusion.140 = (bf16[1,1024,256]{2,1,0:T(8,128)(2,1)S(1)}, bf16[1,1024,256]{2,1,0:T(8,128)(2,1)}) fusion(bf16[2,1024,256]{2,1,0:T(8,128)(2,1)} %collective-permute-done.3), kind=kLoop, calls=%fused_computation.257 | loop fusion | bytes 2097152 | tf_op jit(solution)/shard_map/slice | solution.py:170
  119.1 40.9 %while.7 = (s32[]{:T(128)}, f32[2,512]{1,0:T(2,128)S(1)}, f32[2,512]{1,0:T(2,128)S(1)}, f32[2,512,128]{2,1,0:T(8,128)S(1)}, f32[2,512]{1,0:T(2,128)S(1)}, /*inde...) while((s32[]{:T(128)}, f32[2,512]{1,0:T(2,128)S(1)}, ...), condition=%wide.region_48.49_spmd.clone, body=%wide.region_40.48_spmd.clone.sunk | while | flops 412750080 | bytes 32438260 | solution.py:158
  119.1 1.3 dynamic-slice_bitcast_fusion.3
  122.1 1.0 constant_dynamic-slice_fusion.8
  123.1 7.6 %conditional.13 = ((f32[2,512]{1,0:T(2,128)S(1)}, f32[2,512]{1,0:T(2,128)S(1)}, f32[2,512,128]{2,1,0:T(8,128)S(1)})) conditional(s32[]{:T(128)} %convert_element_type.146, (f32[2,512]{1,0:T(2,128)S(1)}, f32[2,512]{1,0:T(2,128)S(1)}, f32[2,512,128]{2,1,0:T(8,128)S(1)}) %tuple.178, (s32[4,64]{1,0:T(4,128)S(1)}, s32[64]{0:T(128)}, ...), branch_computations={%region_42.42_spmd, %region_43.45_spmd} | conditional | flops 136972288 | bytes 6368544 | solution.py:155
  124.8 1.3 fusion.136
  127.6 1.6 reshape.929
  129.2 1.5 convolution_add_fusion.4
  131.4 0.9 broadcast_compare_fusion.13
  132.4 1.5 fusion.197
  133.9 1.3 copy-done.1
  136.0 3.5 %convolution_add_fusion.13 = f32[2,512,128]{2,1,0:T(8,128)} fusion(f32[2,512,512]{2,1,0:T(8,128)} %copy-done.1, f32[2,512]{1,0:T(2,128)S(1)} %max.79, pred[512,512]{1,0:T(8,128)(4,1)S(1)} %broadcast_compare_fusion.13, f32[2,512,128]{2,1,0:T(8,128)} %get-tuple-element.1226, bf16[512,2,128]{2,1,0:T(2,128)(2,1)S(1)} %reshape.983, ...), kind=kOutput, calls=%fused_computation.103.clone.1 | convolution fusion | flops 137101312 | bytes 3678208 | tf_op jit(solution)/shard_map/while/body/eval_jaxpr/cnr,ncd->crd/dot_general | solution.py:68
  139.5 1.3 dynamic-slice_bitcast_fusion.3
  142.5 1.0 constant_dynamic-slice_fusion.8
  143.6 7.6 %conditional.13 = ((f32[2,512]{1,0:T(2,128)S(1)}, f32[2,512]{1,0:T(2,128)S(1)}, f32[2,512,128]{2,1,0:T(8,128)S(1)})) conditional(s32[]{:T(128)} %convert_element_type.146, (f32[2,512]{1,0:T(2,128)S(1)}, f32[2,512]{1,0:T(2,128)S(1)}, f32[2,512,128]{2,1,0:T(8,128)S(1)}) %tuple.178, (s32[4,64]{1,0:T(4,128)S(1)}, s32[64]{0:T(128)}, ...), branch_computations={%region_42.42_spmd, %region_43.45_spmd} | conditional | flops 136972288 | bytes 6368544 | solution.py:155
  145.3 1.3 fusion.136
  148.0 1.6 reshape.929
  149.6 1.5 convolution_add_fusion.4
  151.9 0.9 broadcast_compare_fusion.13
  152.8 1.5 fusion.197
  154.4 1.3 copy-done.1
  156.4 3.5 %convolution_add_fusion.13 = f32[2,512,128]{2,1,0:T(8,128)} fusion(f32[2,512,512]{2,1,0:T(8,128)} %copy-done.1, f32[2,512]{1,0:T(2,128)S(1)} %max.79, pred[512,512]{1,0:T(8,128)(4,1)S(1)} %broadcast_compare_fusion.13, f32[2,512,128]{2,1,0:T(8,128)} %get-tuple-element.1226, bf16[512,2,128]{2,1,0:T(2,128)(2,1)S(1)} %reshape.983, ...), kind=kOutput, calls=%fused_computation.103.clone.1 | convolution fusion | flops 137101312 | bytes 3678208 | tf_op jit(solution)/shard_map/while/body/eval_jaxpr/cnr,ncd->crd/dot_general | solution.py:68
  159.9 1.3 divide_convert_fusion
  (258 shorter events, 38.0 us)
Async XLA Ops:
  0.0 4.4 %copy-start = (bf16[2048,256]{1,0:T(8,128)(2,1)S(1)}, bf16[2048,256]{1,0:T(8,128)(2,1)}, u32[]{:S(2)}) copy-start(bf16[2048,256]{1,0:T(8,128)(2,1)} %param.26) | copy-start | bytes 3145732
  0.0 6.2 %copy-start.28 = (f32[128]{0:T(128)S(1)}, f32[128]{0:T(128)}, u32[]{:S(2)}) copy-start(f32[128]{0:T(128)} %param.29) | copy-start | bytes 1540
  3.0 4.0 %copy-start.7 = (bf16[128,2048]{1,0:T(8,128)(2,1)S(1)}, bf16[128,2048]{1,0:T(8,128)(2,1)}, u32[]{:S(2)}) copy-start(bf16[128,2048]{1,0:T(8,128)(2,1)} %param.22) | copy-start | bytes 1572868
  3.0 4.0 %copy-start.21 = (f32[2048]{0:T(1024)S(1)}, f32[2048]{0:T(1024)}, u32[]{:S(2)}) copy-start(f32[2048]{0:T(1024)} %param.24) | copy-start | bytes 24580
  3.0 4.0 %copy-start.32 = (bf16[2048,256]{1,0:T(8,128)(2,1)S(1)}, bf16[2048,256]{1,0:T(8,128)(2,1)}, u32[]{:S(2)}) copy-start(bf16[2048,256]{1,0:T(8,128)(2,1)} %param.27) | copy-start | bytes 3145732
  5.9 6.6 %copy-start.24 = (s32[16,2]{0,1:T(2,128)S(1)}, s32[16,2]{0,1:T(2,128)}, u32[]{:S(2)}) copy-start(s32[16,2]{0,1:T(2,128)} %param.23) | copy-start | bytes 388
  7.0 19.0 %copy-start.13 = (bf16[1,128,256]{2,1,0:T(8,128)(2,1)}, bf16[1,128,256]{2,1,0:T(8,128)(2,1)S(1)}, u32[]{:S(2)}) copy-start(bf16[1,128,256]{2,1,0:T(8,128)(2,1)S(1)} %convert_element_type.92) | copy-start | bytes 196612
  7.4 29.3 %copy-start.11 = (bf16[128,256]{1,0:T(8,128)(2,1)}, bf16[128,256]{1,0:T(8,128)(2,1)S(1)}, u32[]{:S(2)}) copy-start(bf16[128,256]{1,0:T(8,128)(2,1)S(1)} %convolution_convert_fusion) | copy-start | bytes 196612
  7.4 28.5 %collective-permute-start = (bf16[2,128,256]{2,1,0:T(8,128)(2,1)S(1)}, bf16[2,128,256]{2,1,0:T(8,128)(2,1)S(1)}, u32[]{:S(2)}, u32[]{:S(2)}) collective-permute-start(bf16[2,128,256]{2,1,0:T(8,128)(2,1)S(1)} %pad_maximum_fusion.2), channel_id=1, source_target_pairs={{0,1},{1,0},{2,3},{3,2},{4,5},{5,4},{6,7},{7,6},{8,9},{9,8},{10,11... | collective-permute-start | bytes 393224 | tf_op jit(solution)/shard_map/ppermute | solution.py:16
  8.1 22.8 %copy-start.26 = (pred[128]{0:T(512)(128)(4,1)}, pred[128]{0:T(512)(128)(4,1)S(1)}, u32[]{:S(2)}) copy-start(pred[128]{0:T(512)(128)(4,1)S(1)} %iota_compare_fusion.6) | copy-start | bytes 388
  15.2 12.9 %copy-start.22 = (s32[64]{0:T(128)}, s32[64]{0:T(128)S(1)}, u32[]{:S(2)}) copy-start(s32[64]{0:T(128)S(1)} %get-tuple-element.1218) | copy-start | bytes 772
  26.0 0.7 copy-start.29
  27.6 2.9 %copy-start.30 = (s32[128]{0:T(128)S(1)}, s32[128]{0:T(128)}, u32[]{:S(2)}) copy-start(s32[128]{0:T(128)} %add_select_fusion.2) | copy-start | bytes 1540
  27.6 5.3 %slice-start = ((bf16[1,128,256]{2,1,0:T(8,128)(2,1)}), bf16[1,64,256]{2,1,0:T(8,128)(2,1)S(1)}, s32[]{:S(2)}) async-start(bf16[1,128,256]{2,1,0:T(8,128)(2,1)} %copy-done.13), calls=%async_computation | async-start | bytes 65536 | tf_op jit(solution)/shard_map/while/body/eval_jaxpr/slice | solution.py:142
  27.6 5.3 %copy-start.31 = (s32[1,64]{1,0:T(1,128)S(1)}, s32[1,64]{1,0:T(1,128)}, u32[]{:S(2)}) copy-start(s32[1,64]{1,0:T(1,128)} %get-tuple-element.876) | copy-start | bytes 772
  30.7 6.0 %copy-start.14 = (bf16[1,128,256]{2,1,0:T(8,128)(2,1)S(1)}, bf16[1,128,256]{2,1,0:T(8,128)(2,1)}, u32[]{:S(2)}) copy-start(bf16[1,128,256]{2,1,0:T(8,128)(2,1)} %copy-done.13) | copy-start | bytes 196612
  31.0 7.0 %copy-start.23 = (f32[2,512]{1,0:T(2,128)}, f32[2,512]{1,0:T(2,128)S(1)}, u32[]{:S(2)}) copy-start(f32[2,512]{1,0:T(2,128)S(1)} %get-tuple-element.884) | copy-start | bytes 12292
  31.6 3.0 %copy-start.27 = (pred[128]{0:T(512)(128)(4,1)S(1)}, pred[128]{0:T(512)(128)(4,1)}, u32[]{:S(2)}) copy-start(pred[128]{0:T(512)(128)(4,1)} %copy-done.26) | copy-start | bytes 388
  37.4 8.1 %collective-permute-start.1 = (bf16[2,256,256]{2,1,0:T(8,128)(2,1)}, bf16[2,256,256]{2,1,0:T(8,128)(2,1)}, u32[]{:S(2)}, u32[]{:S(2)}) collective-permute-start(bf16[2,256,256]{2,1,0:T(8,128)(2,1)} %maximum_select_fusion.2), channel_id=1, source_target_pairs={{0,2},{1,3},{2,0},{3,1},{4,6},{5,7},{6,4},{7,5},{8,10},{9,11},{10,... | collective-permute-start | bytes 786440 | tf_op jit(solution)/shard_map/ppermute | solution.py:16
  37.6 1.2 copy-start.12
  37.6 1.8 %copy-start.16 = (bf16[128,2,128]{2,1,0:T(2,128)(2,1)S(1)}, bf16[128,2,128]{2,1,0:T(2,128)(2,1)}, u32[]{:S(2)}) copy-start(bf16[128,2,128]{2,1,0:T(2,128)(2,1)} %reshape.955) | copy-start | bytes 196612
  47.6 13.6 %collective-permute-start.2 = (bf16[2,512,256]{2,1,0:T(8,128)(2,1)}, bf16[2,512,256]{2,1,0:T(8,128)(2,1)}, u32[]{:S(2)}, u32[]{:S(2)}) collective-permute-start(bf16[2,512,256]{2,1,0:T(8,128)(2,1)} %maximum_select_fusion.1), channel_id=1, source_target_pairs={{0,4},{1,5},{2,6},{3,7},{4,0},{5,1},{6,2},{7,3},{8,12},{9,13},{10,... | collective-permute-start | bytes 1572872 | tf_op jit(solution)/shard_map/ppermute | solution.py:16
  61.2 5.5 %copy-start.19 = (f32[2,512]{1,0:T(2,128)}, f32[2,512]{1,0:T(2,128)S(1)}, u32[]{:S(2)}) copy-start(f32[2,512]{1,0:T(2,128)S(1)} %get-tuple-element.492) | copy-start | bytes 12292
  61.2 9.7 %copy-start.9 = (pred[512,512]{1,0:T(8,128)(4,1)S(1)}, pred[512,512]{1,0:T(8,128)(4,1)}, u32[]{:S(2)}) copy-start(pred[512,512]{1,0:T(8,128)(4,1)} %broadcast_compare_fusion.7) | copy-start | bytes 786436
  63.9 7.1 %copy-start.15 = (bf16[512,2,128]{2,1,0:T(2,128)(2,1)S(1)}, bf16[512,2,128]{2,1,0:T(2,128)(2,1)}, u32[]{:S(2)}) copy-start(bf16[512,2,128]{2,1,0:T(2,128)(2,1)} %reshape.956) | copy-start | bytes 786436
  63.9 9.0 %copy-start.25 = (s32[4,64]{1,0:T(4,128)S(1)}, s32[4,64]{1,0:T(4,128)}, u32[]{:S(2)}) copy-start(s32[4,64]{1,0:T(4,128)} %get-tuple-element.861) | copy-start | bytes 3076
  66.7 50.3 %collective-permute-start.3 = (bf16[2,1024,256]{2,1,0:T(8,128)(2,1)}, bf16[2,1024,256]{2,1,0:T(8,128)(2,1)}, u32[]{:S(2)}, u32[]{:S(2)}) collective-permute-start(bf16[2,1024,256]{2,1,0:T(8,128)(2,1)} %maximum_select_fusion), channel_id=1, source_target_pairs={{0,8},{1,9},{2,10},{3,11},{4,12},{5,13},{6,14},{7,15},{8,0},{9,1},... | collective-permute-start | bytes 3145736 | tf_op jit(solution)/shard_map/ppermute | solution.py:16
  73.2 2.3 %copy-start.20 = (f32[2,512]{1,0:T(2,128)S(1)}, f32[2,512]{1,0:T(2,128)}, u32[]{:S(2)}) copy-start(f32[2,512]{1,0:T(2,128)} %copy-done.19) | copy-start | bytes 12292
  73.2 3.0 %copy-start.10 = (pred[512,512]{1,0:T(8,128)(4,1)S(1)}, pred[512,512]{1,0:T(8,128)(4,1)}, u32[]{:S(2)}) copy-start(pred[512,512]{1,0:T(8,128)(4,1)} %broadcast_compare_fusion.7) | copy-start | bytes 786436
  73.2 2.9 %copy-start.8 = (f32[2,512,512]{2,1,0:T(8,128)S(1)}, f32[2,512,512]{2,1,0:T(8,128)}, u32[]{:S(2)}) copy-start(f32[2,512,512]{2,1,0:T(8,128)} %get-tuple-element.889) | copy-start | bytes 6291460
  119.1 4.0 %copy-start.2 = (bf16[2,512,128]{2,1,0:T(8,128)(2,1)}, bf16[2,512,128]{2,1,0:T(8,128)(2,1)S(1)}, u32[]{:S(2)}) copy-start(bf16[2,512,128]{2,1,0:T(8,128)(2,1)S(1)} %get-tuple-element.1248) | copy-start | bytes 786436 | tf_op jit(solution)/shard_map/while
  119.1 4.0 %copy-start.5 = (bf16[2,4,128,256]{3,2,1,0:T(8,128)(2,1)}, bf16[2,4,128,256]{3,2,1,0:T(8,128)(2,1)S(1)}, u32[]{:S(2)}) copy-start(bf16[2,4,128,256]{3,2,1,0:T(8,128)(2,1)S(1)} %get-tuple-element.1246) | copy-start | bytes 1572868 | tf_op jit(solution)/shard_map/while
  132.4 3.5 %copy-start.17 = (f32[2,512]{1,0:T(2,128)S(1)}, f32[2,512]{1,0:T(2,128)}, u32[]{:S(2)}) copy-start(f32[2,512]{1,0:T(2,128)} %get-tuple-element.1225) | copy-start | bytes 12292 | tf_op jit(solution)/shard_map/while
  133.9 1.4 copy-start.1
  135.8 3.6 %copy-start.18 = (f32[2,512]{1,0:T(2,128)}, f32[2,512]{1,0:T(2,128)S(1)}, u32[]{:S(2)}) copy-start(f32[2,512]{1,0:T(2,128)S(1)} %get-tuple-element.1241) | copy-start | bytes 12292 | tf_op jit(solution)/shard_map/while
  135.9 3.5 %copy-start.3 = (bf16[2,512,128]{2,1,0:T(8,128)(2,1)S(1)}, bf16[2,512,128]{2,1,0:T(8,128)(2,1)}, u32[]{:S(2)}) copy-start(bf16[2,512,128]{2,1,0:T(8,128)(2,1)} %copy-done.2) | copy-start | bytes 786436 | tf_op jit(solution)/shard_map/while
  135.9 3.5 %copy-start.6 = (bf16[2,4,128,256]{3,2,1,0:T(8,128)(2,1)S(1)}, bf16[2,4,128,256]{3,2,1,0:T(8,128)(2,1)}, u32[]{:S(2)}) copy-start(bf16[2,4,128,256]{3,2,1,0:T(8,128)(2,1)} %copy-done.5) | copy-start | bytes 1572868 | tf_op jit(solution)/shard_map/while
  139.5 4.1 %copy-start.2 = (bf16[2,512,128]{2,1,0:T(8,128)(2,1)}, bf16[2,512,128]{2,1,0:T(8,128)(2,1)S(1)}, u32[]{:S(2)}) copy-start(bf16[2,512,128]{2,1,0:T(8,128)(2,1)S(1)} %get-tuple-element.1248) | copy-start | bytes 786436 | tf_op jit(solution)/shard_map/while
  139.5 4.1 %copy-start.5 = (bf16[2,4,128,256]{3,2,1,0:T(8,128)(2,1)}, bf16[2,4,128,256]{3,2,1,0:T(8,128)(2,1)S(1)}, u32[]{:S(2)}) copy-start(bf16[2,4,128,256]{3,2,1,0:T(8,128)(2,1)S(1)} %get-tuple-element.1246) | copy-start | bytes 1572868 | tf_op jit(solution)/shard_map/while
  152.8 3.5 %copy-start.17 = (f32[2,512]{1,0:T(2,128)S(1)}, f32[2,512]{1,0:T(2,128)}, u32[]{:S(2)}) copy-start(f32[2,512]{1,0:T(2,128)} %get-tuple-element.1225) | copy-start | bytes 12292 | tf_op jit(solution)/shard_map/while
  154.3 1.4 copy-start.1
  156.3 3.6 %copy-start.18 = (f32[2,512]{1,0:T(2,128)}, f32[2,512]{1,0:T(2,128)S(1)}, u32[]{:S(2)}) copy-start(f32[2,512]{1,0:T(2,128)S(1)} %get-tuple-element.1241) | copy-start | bytes 12292 | tf_op jit(solution)/shard_map/while
  156.4 3.5 %copy-start.3 = (bf16[2,512,128]{2,1,0:T(8,128)(2,1)S(1)}, bf16[2,512,128]{2,1,0:T(8,128)(2,1)}, u32[]{:S(2)}) copy-start(bf16[2,512,128]{2,1,0:T(8,128)(2,1)} %copy-done.2) | copy-start | bytes 786436 | tf_op jit(solution)/shard_map/while
  156.4 3.5 %copy-start.6 = (bf16[2,4,128,256]{3,2,1,0:T(8,128)(2,1)S(1)}, bf16[2,4,128,256]{3,2,1,0:T(8,128)(2,1)}, u32[]{:S(2)}) copy-start(bf16[2,4,128,256]{3,2,1,0:T(8,128)(2,1)} %copy-done.5) | copy-start | bytes 1572868 | tf_op jit(solution)/shard_map/while
where the time goes:
time: 164 us; the launch traced here: 163 us
  waiting for transfers between devices  44 us (27%)
  other arithmetic  35 us (21%)
  local copies, waits for them, and re-layouts  32.5 us (20%)
  matrix products  31 us (19%)
  between operations  8.15 us (5%)
  starting transfers between devices  6.53 us (4%)
  loops' own time  5.71 us (3%)
    ppermute x4, waiting for transfers between devices, partner(): lax.ppermute(x, axis, [(i, i ^ 1 << bit) for i in range(lax.axis_size(axi...  44 us
    dot_general x11, matrix products, update(): jnp.einsum('cnr,ncd->crd', weight.astype(jnp.bfloat16), values_three, pre...  15.5 us
    dot_general x11, matrix products, update(): jnp.einsum('ncd,crd->cnr', keys_three, rows_query, preferred_element_type...  9 us
    ppermute x4, starting transfers between devices, partner(): lax.ppermute(x, axis, [(i, i ^ 1 << bit) for i in range(lax.axis_size(axi...  6.53 us
    slice x7, other arithmetic, advance(): early_keypos = block_position[:, :half_rows].reshape(-1)  6.37 us
    select_n x3, other arithmetic, body(): jnp.where(upper_half, jnp.concatenate([received, holding], axis=1), jnp.c...  5.68 us
    le x15, local copies, waits for them, and re-layouts, update(): visible = (block_position[:, None] <= rows_position[None, :])[None]  5.32 us
    another operation x2, loops' own time, absorb(): lax.scan(advance, carried, (keys_grouped, values_grouped, position_grouped))  5.2 us
  transfers between devices with their start and end apart: 4, of which 2 were waited for; matrix products, arithmetic and copies ran while one was open for 25% of the time, Pallas kernels for 0%

commit v1 on v0

v1 whole, which is shorter than its diff:
```python
import functools

import jax
import jax.numpy as jnp
import numpy as np
from jax import lax
from jax.experimental import pallas as pl
from jax.experimental.pallas import tpu as pltpu
from jax.sharding import PartitionSpec as P

HEAD = 128
EPSILON = 1e-06
THETA = 1000000.0
MESH = pl.DeviceIdType.MESH
LOW = -1e30
FACTOR = HEAD ** (-0.5) * 1.4426950408889634
F32 = jnp.float32
BF16 = jnp.bfloat16


def flip(index, mask):
    for bit in range(mask.bit_length()):
        if mask >> bit & 1:
            index = index + (1 << bit) * (1 - 2 * ((index // (1 << bit)) % 2))
    return index


def kernel(
    n, heads, kv_heads,
    hidden_ref, span_ref, gain_ref, wq_hbm, wk_hbm, wv_hbm, qgain_ref, kgain_ref, inverse_ref,
    out_ref,
    wq_ref, wk_ref, wv_ref, kv_ref, q_ref, s_ref, vta_ref, vtb_ref, vtc_ref, pa_ref, pb_ref,
    acc_ref, peak_ref, total_ref,
    w_sem, recv_sem, z_sem, y_sem, c_sem,
):
    rows = hidden_ref.shape[0]
    half = rows // 2
    group = heads // kv_heads
    wide = group * half
    me = lax.axis_index("ctx")
    lanes_z = n // 4
    z, y, c = me // 4, (me // 2) % 2, me % 2

    def ident(zz, yy, cc):
        return zz * 4 + yy * 2 + cc

    def place(step, k):
        return 4 * ((z // 4 + step) % (lanes_z // 4)) + flip(z % 4, k)

    y_peer = ident(z, 1 - y, c)
    c_peer = ident(z, y, 1 - c)

    chunk = 4 * HEAD
    chunks = heads * HEAD // chunk
    load_k = pltpu.make_async_copy(wk_hbm, wk_ref, w_sem.at[0])
    load_v = pltpu.make_async_copy(wv_hbm, wv_ref, w_sem.at[1])
    load_q = [
        pltpu.make_async_copy(
            wq_hbm.at[:, pl.ds(i * chunk, chunk)], wq_ref.at[i], w_sem.at[2 + i]
        )
        for i in range(chunks)
    ]
    load_k.start()
    load_v.start()
    for copy in load_q:
        copy.start()

    barrier = pltpu.get_barrier_semaphore()
    others = [(s, k) for s in range(lanes_z // 4) for k in range(4) if (s, k) != (0, 0)]
    for peer in [y_peer, c_peer] + [ident(place(s, k), y, c) for s, k in others]:
        pl.semaphore_signal(barrier, inc=1, device_id={"ctx": peer}, device_id_type=MESH)

    def send(src, target, sem):
        return pltpu.make_async_remote_copy(
            src_ref=kv_ref.at[src],
            dst_ref=kv_ref.at[src],
            send_sem=sem,
            recv_sem=recv_sem.at[src],
            device_id={"ctx": target},
            device_id_type=MESH,
        )

    def arrived(src):
        send(src, c_peer, c_sem.at[0]).wait_recv()

    hidden = hidden_ref[...].astype(F32)
    mean_square = jnp.mean(hidden * hidden, axis=-1, keepdims=True)
    normed = (hidden * lax.rsqrt(mean_square + EPSILON) * gain_ref[...]).astype(BF16)

    own_first, own_second = span_ref[me, 0], span_ref[me, 1]
    within = lax.broadcasted_iota(jnp.int32, (rows, HEAD), 0)
    position = jnp.where(
        within < half, own_first * half + within, own_second * half + within - half
    )
    angles = position.astype(F32) * inverse_ref[...]
    cosine = jnp.cos(angles)
    sine = jnp.sin(angles)
    lane = lax.broadcasted_iota(jnp.int32, (rows, HEAD), 1)
    sine = jnp.where(lane < HEAD // 2, -sine, sine)

    def finished(entries, gains):
        square = jnp.mean(entries * entries, axis=-1, keepdims=True)
        entries = entries * lax.rsqrt(square + EPSILON) * gains
        return (entries * cosine + pltpu.roll(entries, HEAD // 2, 1) * sine).astype(BF16)

    load_k.wait()
    keys = jnp.dot(normed, wk_ref[...], preferred_element_type=F32)
    for g in range(kv_heads):
        cut = slice(g * HEAD, (g + 1) * HEAD)
        kv_ref[me, 0, :, cut] = finished(keys[:, cut], kgain_ref[...])
    load_v.wait()
    kv_ref[me, 1] = jnp.dot(normed, wv_ref[...], preferred_element_type=F32).astype(BF16)

    pl.semaphore_wait(barrier, 2 + len(others))
    send(me, c_peer, c_sem.at[0]).start()
    send(me, y_peer, y_sem.at[0]).start()
    for i, (s, k) in enumerate(others):
        send(me, ident(place(s, k), y, c), z_sem.at[i]).start()

    ordered = own_first < own_second
    own_low = jnp.minimum(own_first, own_second)
    for i in range(chunks):
        load_q[i].wait()
        part = jnp.dot(normed, wq_ref[i], preferred_element_type=F32)
        for j in range(chunk // HEAD):
            head = i * (chunk // HEAD) + j
            done = finished(part[:, j * HEAD:(j + 1) * HEAD], qgain_ref[...])
            g, r = head // group, head % group
            first, second = done[:half], done[half:]
            q_ref[g, r * half:(r + 1) * half, :HEAD] = jnp.where(ordered, first, second)
            q_ref[g, r * half:(r + 1) * half, HEAD:] = jnp.where(ordered, second, first)

    def transposed_dot(a, b):
        return lax.dot_general(a, b, (((1,), (1,)), ((), ())), preferred_element_type=F32)

    def block_peak(block):
        tall = block.shape[0]
        return jnp.max(block.reshape(tall // 8, 8, wide), axis=0)

    visible = (
        lax.broadcasted_iota(jnp.int32, (half, wide), 0)
        <= lax.broadcasted_iota(jnp.int32, (half, wide), 1) % half
    )

    def score(zz, k, own, peaks):
        sources = []
        for yy, cc in ((y, c), (y, 1 - c), (1 - y, c), (1 - y, 1 - c)):
            src = ident(zz, yy, cc)
            upper = span_ref[src, 0] > span_ref[src, 1]
            early = jnp.minimum(span_ref[src, 0], span_ref[src, 1]) < own_low
            sources.append((src, upper, early))
        for g in range(kv_heads):
            cut = slice(g * HEAD, (g + 1) * HEAD)

            def piece(src, part, upper):
                first = kv_ref[src, part, :half, cut]
                second = kv_ref[src, part, half:, cut]
                return jnp.where(upper, second, first)

            span = slice(k * 4 * half, (k + 1) * 4 * half)
            low_keys = jnp.concatenate([piece(s, 0, up) for s, up, e in sources], axis=0)
            scores = transposed_dot(low_keys, q_ref[g, :, HEAD:])
            s_ref[g, 0, span, :] = scores
            peaks[g][1] = jnp.maximum(peaks[g][1], block_peak(scores))
            low_values = jnp.concatenate([piece(s, 1, up) for s, up, e in sources], axis=0)
            vta_ref[g, :, span] = low_values.T

            def parted(part):
                early_side, late_side = [], []
                for src, upper, early in sources:
                    block = piece(src, part, upper == early)
                    early_side.append(jnp.where(early, block, jnp.zeros_like(block)))
                    late_side.append(jnp.where(early, jnp.zeros_like(block), block))
                return jnp.concatenate(
                    [jnp.concatenate(early_side, axis=0), jnp.concatenate(late_side, axis=0)],
                    axis=1,
                )

            mixed = transposed_dot(parted(0), q_ref[g])
            for j, (src, upper, early) in enumerate(sources):
                scores = mixed[j * half:(j + 1) * half]
                if own and j == 0:
                    scores = jnp.where(visible, scores, LOW)
                at = (k * 4 + j) * half
                s_ref[g, 1, at:at + half, :] = scores
                peak = block_peak(scores)
                peaks[g][0] = jnp.maximum(peaks[g][0], jnp.where(early, peak, LOW))
                peaks[g][1] = jnp.maximum(peaks[g][1], jnp.where(early, LOW, peak))
            vtb_ref[g, :, span] = parted(1).T
            if own:
                src, upper, early = sources[0]
                scores = transposed_dot(piece(src, 0, upper), q_ref[g, :, :HEAD])
                scores = jnp.where(visible, scores, LOW)
                s_ref[g, 1, 16 * half:17 * half, :] = scores
                peaks[g][0] = jnp.maximum(peaks[g][0], block_peak(scores))
                vtc_ref[g] = piece(src, 1, upper).T

    def take(step, k):
        i = step * 4 + k
        src = ident(place(step, k), y, c)
        arrived(src)
        send(src, y_peer, y_sem.at[i]).start()
        send(src, c_peer, c_sem.at[2 * i]).start()

    def pass_on(step, k):
        i = step * 4 + k
        src = ident(place(step, k), 1 - y, c)
        arrived(src)
        send(src, c_peer, c_sem.at[2 * i + 1]).start()

    def last(step, k):
        arrived(ident(place(step, k), y, 1 - c))
        arrived(ident(place(step, k), 1 - y, 1 - c))

    def sums(block):
        tall = block.shape[0]
        return jnp.sum(block.reshape(tall // 8, 8, wide), axis=0)

    def absorb(step, first, peaks):
        for g in range(kv_heads):
            new = [jnp.max(peaks[g][t], axis=0, keepdims=True) for t in range(2)]
            if not first:
                new = [jnp.maximum(new[t], peak_ref[g, t]) for t in range(2)]
            totals = [jnp.zeros((8, wide), F32), jnp.zeros((8, wide), F32)]
            for k in range(4):
                at = k * 4 * half
                weight = jnp.exp2((s_ref[g, 0, at:at + 4 * half, :] - new[1]) * FACTOR)
                totals[1] = totals[1] + sums(weight)
                pa_ref[at:at + 4 * half, :] = weight.astype(BF16)
                for j, (yy, cc) in enumerate(
                    ((y, c), (y, 1 - c), (1 - y, c), (1 - y, 1 - c))
                ):
                    src = ident(place(step, k), yy, cc)
                    early = jnp.minimum(span_ref[src, 0], span_ref[src, 1]) < own_low
                    spot = at + j * half
                    peak = jnp.where(early, new[0], new[1])
                    weight = jnp.exp2((s_ref[g, 1, spot:spot + half, :] - peak) * FACTOR)
                    part = sums(weight)
                    totals[0] = totals[0] + jnp.where(early, part, 0.0)
                    totals[1] = totals[1] + jnp.where(early, 0.0, part)
                    pb_ref[spot:spot + half, :] = weight.astype(BF16)
            mixed = jnp.dot(vtb_ref[g], pb_ref[...], preferred_element_type=F32)
            added = [
                mixed[:HEAD],
                mixed[HEAD:] + jnp.dot(vta_ref[g], pa_ref[...], preferred_element_type=F32),
            ]
            if first:
                weight = jnp.exp2((s_ref[g, 1, 16 * half:17 * half, :] - new[0]) * FACTOR)
                totals[0] = totals[0] + sums(weight)
                added[0] = added[0] + jnp.dot(
                    vtc_ref[g], weight.astype(BF16), preferred_element_type=F32
                )
            for t in range(2):
                total = jnp.sum(totals[t], axis=0, keepdims=True)
                if first:
                    acc_ref[g, t] = added[t]
                    total_ref[g, t] = total
                else:
                    decay = jnp.exp2((peak_ref[g, t] - new[t]) * FACTOR)
                    acc_ref[g, t] = acc_ref[g, t] * decay + added[t]
                    total_ref[g, t] = total_ref[g, t] * decay + total
                peak_ref[g, t] = new[t]

    def nothing():
        return [[jnp.full((8, wide), LOW, F32) for t in range(2)] for g in range(kv_heads)]

    peaks = nothing()
    arrived(c_peer)
    pass_on(0, 0)
    take(0, 1)
    arrived(ident(z, 1 - y, 1 - c))
    score(z, 0, True, peaks)
    take(0, 2)
    pass_on(0, 1)
    take(0, 3)
    last(0, 1)
    score(place(0, 1), 1, False, peaks)
    pass_on(0, 2)
    last(0, 2)
    score(place(0, 2), 2, False, peaks)
    pass_on(0, 3)
    last(0, 3)
    score(place(0, 3), 3, False, peaks)
    absorb(0, True, peaks)

    def further(step, carry):
        peaks = nothing()
        for k in range(4):
            take(step, k)
        for k in range(4):
            pass_on(step, k)
        for k in range(4):
            last(step, k)
            score(place(step, k), k, False, peaks)
        absorb(step, False, peaks)
        return carry

    if lanes_z > 4:
        lax.fori_loop(1, lanes_z // 4, further, 0)

    for g in range(kv_heads):
        low = acc_ref[g, 0] / total_ref[g, 0]
        high = acc_ref[g, 1] / total_ref[g, 1]
        for r in range(0, group, 2):
            low_rows = low[:, r * half:(r + 2) * half].T
            high_rows = high[:, r * half:(r + 2) * half].T
            first = jnp.where(ordered, low_rows, high_rows).astype(BF16)
            second = jnp.where(ordered, high_rows, low_rows).astype(BF16)
            for e in range(2):
                at = (g * group + r + e) * HEAD
                out_ref[:half, at:at + HEAD] = first[e * half:(e + 1) * half]
                out_ref[half:, at:at + HEAD] = second[e * half:(e + 1) * half]

    for i in range(len(others)):
        send(me, y_peer, z_sem.at[i]).wait_send()
    for i in range(lanes_z):
        send(me, y_peer, y_sem.at[i]).wait_send()
    for i in range(2 * lanes_z):
        send(me, y_peer, c_sem.at[i]).wait_send()


def solution(mesh):
    n = mesh.shape["ctx"]

    def body(hidden_in, span_order, norm_gain, w_query, w_key, w_value, query_gain, key_gain):
        rows, depth = hidden_in.shape
        heads, kv_heads = w_query.shape[1] // HEAD, w_key.shape[1] // HEAD
        half = rows // 2
        wide = heads // kv_heads * half
        frequency = THETA ** (-np.arange(HEAD // 2, dtype=np.float64) * (2.0 / HEAD))
        inverse = jnp.asarray(np.tile(frequency, 2)[None, :], F32)
        vmem = pl.BlockSpec(memory_space=pltpu.VMEM)
        anywhere = pl.BlockSpec(memory_space=pl.ANY)
        chunk = 4 * HEAD
        chunks = heads * HEAD // chunk
        return pl.pallas_call(
            functools.partial(kernel, n, heads, kv_heads),
            out_shape=jax.ShapeDtypeStruct((rows, heads * HEAD), BF16),
            in_specs=[
                vmem, pl.BlockSpec(memory_space=pltpu.SMEM), vmem,
                anywhere, anywhere, anywhere, vmem, vmem, vmem,
            ],
            out_specs=vmem,
            scratch_shapes=[
                pltpu.VMEM((chunks, depth, chunk), BF16),
                pltpu.VMEM((depth, kv_heads * HEAD), BF16),
                pltpu.VMEM((depth, kv_heads * HEAD), BF16),
                pltpu.VMEM((n, 2, rows, kv_heads * HEAD), BF16),
                pltpu.VMEM((kv_heads, wide, 2 * HEAD), BF16),
                pltpu.VMEM((kv_heads, 2, 17 * half, wide), F32),
                pltpu.VMEM((kv_heads, HEAD, 16 * half), BF16),
                pltpu.VMEM((kv_heads, 2 * HEAD, 16 * half), BF16),
                pltpu.VMEM((kv_heads, HEAD, half), BF16),
                pltpu.VMEM((16 * half, wide), BF16),
                pltpu.VMEM((16 * half, wide), BF16),
                pltpu.VMEM((kv_heads, 2, HEAD, wide), F32),
                pltpu.VMEM((kv_heads, 2, 1, wide), F32),
                pltpu.VMEM((kv_heads, 2, 1, wide), F32),
                pltpu.SemaphoreType.DMA((2 + chunks,)),
                pltpu.SemaphoreType.DMA((n,)),
                pltpu.SemaphoreType.DMA((n // 4,)),
                pltpu.SemaphoreType.DMA((n // 4,)),
                pltpu.SemaphoreType.DMA((n // 2,)),
            ],
            compiler_params=pltpu.CompilerParams(
                collective_id=0, has_side_effects=True, vmem_limit_bytes=60 * 1024 * 1024
            ),
        )(
            hidden_in, span_order, norm_gain.reshape(1, -1), w_query, w_key, w_value,
            query_gain.reshape(1, -1), key_gain.reshape(1, -1), inverse,
        )

    in_specs = (P(("groups", "ctx"), None), P("groups", None), P(), P(), P(), P(), P(), P())
    out_specs = P(("groups", "ctx"), None)
    return jax.shard_map(body, mesh=mesh, in_specs=in_specs, out_specs=out_specs, check_vma=False)
```

time: 164 us -> 30.8 us (0.19)
  the two profiles are of different devices: /device:TPU:7 before, /device:TPU:1 now
where the time goes in v1:
time: 30.8 us; the launch traced here: 30.6 us
  Pallas kernels  27.4 us (89%)
  local copies, waits for them, and re-layouts  3.23 us (10%)
    pallas_call x1, Pallas kernels, body(): pl.pallas_call(functools.partial(kernel, n, heads, kv_heads), out_shape=j...  27.4 us
    unnamed x2, local copies, waits for them, and re-layouts  3.23 us

profile of v1, /device:TPU:1, one launch (start us, length us, event | category | flops | bytes accessed | tf_op | source)
XLA Modules:
  0.0 30.6 jit_solution(17036906621047974309)
XLA Ops:
  0.0 1.4 %copy.10.span_ref = s32[16,2]{1,0:T(8,128)} copy(s32[16,2]{0,1:T(2,128)} %param.10) | data formatting | bytes 256 | tf_op args[1]
  1.4 27.4 %shard_map.91 = bf16[128,2048]{1,0:T(8,128)(2,1)} custom-call(bf16[128,2048]{1,0:T(8,128)(2,1)} %hidden_ref.1, s32[16,2]{1,0:T(8,128)} %copy.10.span_ref, f32[1,2048]{1,0:T(1,128)} %bitcast.3, bf16[2048,2048]{1,0:T(8,128)(2,1)} %wq_hbm.1, bf16[2048,256]{1,0:T(8,128)(2,1)} %wk_hbm.1, bf16[2048,256]{1,0:T(8,128)(2,1)} %wv_hbm.1, f32[1,128]{1,0:T(1,128)} %bitcast.4, ...), custom_call_target="tpu_custom_call" | custom-call | tf_op jit(solution)/shard_map/pallas_call | solution.py:336
  28.7 1.9 %copy.12 = bf16[128,2048]{1,0:T(8,128)(2,1)} copy(bf16[128,2048]{1,0:T(8,128)(2,1)} %shard_map.91) | data formatting | bytes 1048576

commit v2 on v1

--- a/solution.py
+++ b/solution.py
@@ -27,11 +27,11 @@
 
 def kernel(
     n, heads, kv_heads,
-    hidden_ref, span_ref, gain_ref, wq_hbm, wk_hbm, wv_hbm, qgain_ref, kgain_ref, inverse_ref,
+    hidden_hbm, span_ref, gain_ref, wq_hbm, wk_hbm, wv_hbm, qgain_ref, kgain_ref, inverse_ref,
     out_ref,
-    wq_ref, wk_ref, wv_ref, kv_ref, q_ref, s_ref, vta_ref, vtb_ref, vtc_ref, pa_ref, pb_ref,
+    hidden_ref, wq_ref, wk_ref, wv_ref, kv_ref, q_ref, s_ref, vta_ref, vtb_ref, vtc_ref, pa_ref, pb_ref,
     acc_ref, peak_ref, total_ref,
-    w_sem, recv_sem, z_sem, y_sem, c_sem,
+    w_sem, recv_sem, up_sem, down_sem, y_sem, c_sem,
 ):
     rows = hidden_ref.shape[0]
     half = rows // 2
@@ -60,34 +60,54 @@
         )
         for i in range(chunks)
     ]
+    load_h = pltpu.make_async_copy(hidden_hbm, hidden_ref, w_sem.at[2 + chunks])
+    load_h.start()
     load_k.start()
     load_v.start()
-    for copy in load_q:
-        copy.start()
 
     barrier = pltpu.get_barrier_semaphore()
-    others = [(s, k) for s in range(lanes_z // 4) for k in range(4) if (s, k) != (0, 0)]
-    for peer in [y_peer, c_peer] + [ident(place(s, k), y, c) for s, k in others]:
+    below, above = z > 0, z < lanes_z - 1
+
+    def greet(peer):
         pl.semaphore_signal(barrier, inc=1, device_id={"ctx": peer}, device_id_type=MESH)
 
-    def send(src, target, sem):
+    greet(y_peer)
+    greet(c_peer)
+    pl.when(below)(lambda: greet(me - 4))
+    pl.when(above)(lambda: greet(me + 4))
+
+    def send(src, p, target, sem):
         return pltpu.make_async_remote_copy(
-            src_ref=kv_ref.at[src],
-            dst_ref=kv_ref.at[src],
+            src_ref=kv_ref.at[src, p],
+            dst_ref=kv_ref.at[src, p],
             send_sem=sem,
-            recv_sem=recv_sem.at[src],
+            recv_sem=recv_sem.at[src, p],
             device_id={"ctx": target},
             device_id_type=MESH,
         )
 
-    def arrived(src):
-        send(src, c_peer, c_sem.at[0]).wait_recv()
-
-    hidden = hidden_ref[...].astype(F32)
-    mean_square = jnp.mean(hidden * hidden, axis=-1, keepdims=True)
-    normed = (hidden * lax.rsqrt(mean_square + EPSILON) * gain_ref[...]).astype(BF16)
-
-    own_first, own_second = span_ref[me, 0], span_ref[me, 1]
+    def arrived(src, p):
+        send(src, p, c_peer, c_sem.at[0, p]).wait_recv()
+
+    def to_y(zz, p):
+        return send(ident(zz, y, c), p, y_peer, y_sem.at[zz, p])
+
+    def to_core(zz, yy, p):
+        return send(ident(zz, yy, c), p, c_peer, c_sem.at[2 * zz + yy, p])
+
+    def to_above(zz, p):
+        return send(ident(zz, y, c), p, me + 4, up_sem.at[zz, p])
+
+    def to_below(zz, p):
+        return send(ident(zz, y, c), p, me - 4, down_sem.at[zz, p])
+
+    def publish(p):
+        to_core(z, y, p).start()
+        to_y(z, p).start()
+        pl.when(above)(lambda: to_above(z, p).start())
+        pl.when(below)(lambda: to_below(z, p).start())
+
+    own_first, own_second = span_ref[0, me], span_ref[1, me]
     within = lax.broadcasted_iota(jnp.int32, (rows, HEAD), 0)
     position = jnp.where(
         within < half, own_first * half + within, own_second * half + within - half
@@ -103,23 +123,27 @@
         entries = entries * lax.rsqrt(square + EPSILON) * gains
         return (entries * cosine + pltpu.roll(entries, HEAD // 2, 1) * sine).astype(BF16)
 
+    load_h.wait()
+    hidden = hidden_ref[...].astype(F32)
+    mean_square = jnp.mean(hidden * hidden, axis=-1, keepdims=True)
+    normed = (hidden * lax.rsqrt(mean_square + EPSILON) * gain_ref[...]).astype(BF16)
+
     load_k.wait()
+    load_v.wait()
+    for copy in load_q:
+        copy.start()
     keys = jnp.dot(normed, wk_ref[...], preferred_element_type=F32)
     for g in range(kv_heads):
         cut = slice(g * HEAD, (g + 1) * HEAD)
         kv_ref[me, 0, :, cut] = finished(keys[:, cut], kgain_ref[...])
-    load_v.wait()
+    pl.semaphore_wait(barrier, 2 + jnp.where(below, 1, 0) + jnp.where(above, 1, 0))
+    publish(0)
     kv_ref[me, 1] = jnp.dot(normed, wv_ref[...], preferred_element_type=F32).astype(BF16)
-
-    pl.semaphore_wait(barrier, 2 + len(others))
-    send(me, c_peer, c_sem.at[0]).start()
-    send(me, y_peer, y_sem.at[0]).start()
-    for i, (s, k) in enumerate(others):
-        send(me, ident(place(s, k), y, c), z_sem.at[i]).start()
+    publish(1)
 
     ordered = own_first < own_second
     own_low = jnp.minimum(own_first, own_second)
-    for i in range(chunks):
+    def query(i):
         load_q[i].wait()
         part = jnp.dot(normed, wq_ref[i], preferred_element_type=F32)
         for j in range(chunk // HEAD):
@@ -146,8 +170,8 @@
         sources = []
         for yy, cc in ((y, c), (y, 1 - c), (1 - y, c), (1 - y, 1 - c)):
             src = ident(zz, yy, cc)
-            upper = span_ref[src, 0] > span_ref[src, 1]
-            early = jnp.minimum(span_ref[src, 0], span_ref[src, 1]) < own_low
+            upper = span_ref[0, src] > span_ref[1, src]
+            early = jnp.minimum(span_ref[0, src], span_ref[1, src]) < own_low
             sources.append((src, upper, early))
         for g in range(kv_heads):
             cut = slice(g * HEAD, (g + 1) * HEAD)
@@ -195,34 +219,43 @@
                 peaks[g][0] = jnp.maximum(peaks[g][0], block_peak(scores))
                 vtc_ref[g] = piece(src, 1, upper).T
 
-    def take(step, k):
-        i = step * 4 + k
-        src = ident(place(step, k), y, c)
-        arrived(src)
-        send(src, y_peer, y_sem.at[i]).start()
-        send(src, c_peer, c_sem.at[2 * i]).start()
-
-    def pass_on(step, k):
-        i = step * 4 + k
-        src = ident(place(step, k), 1 - y, c)
-        arrived(src)
-        send(src, c_peer, c_sem.at[2 * i + 1]).start()
-
-    def last(step, k):
-        arrived(ident(place(step, k), y, 1 - c))
-        arrived(ident(place(step, k), 1 - y, 1 - c))
+    def forward(t, p):
+        def from_below():
+            arrived(me - 4 * t, p)
+            pl.when(above)(lambda: to_above(z - t, p).start())
+            to_y(z - t, p).start()
+            to_core(z - t, y, p).start()
+
+        def from_above():
+            arrived(me + 4 * t, p)
+            pl.when(below)(lambda: to_below(z + t, p).start())
+            to_y(z + t, p).start()
+            to_core(z + t, y, p).start()
+
+        pl.when(z >= t)(from_below)
+        pl.when(z + t < lanes_z)(from_above)
+
+    def pass_on(zz, p):
+        arrived(ident(zz, 1 - y, c), p)
+        to_core(zz, 1 - y, p).start()
+
+    def last(zz):
+        for p in range(2):
+            arrived(ident(zz, y, 1 - c), p)
+            arrived(ident(zz, 1 - y, 1 - c), p)
 
     def sums(block):
         tall = block.shape[0]
         return jnp.sum(block.reshape(tall // 8, 8, wide), axis=0)
 
-    def absorb(step, first, peaks):
-        for g in range(kv_heads):
+    def absorb(g, step, parts, first, peaks):
+        span = slice(parts[0] * 4 * half, (parts[-1] + 1) * 4 * half)
+        if True:
             new = [jnp.max(peaks[g][t], axis=0, keepdims=True) for t in range(2)]
             if not first:
                 new = [jnp.maximum(new[t], peak_ref[g, t]) for t in range(2)]
             totals = [jnp.zeros((8, wide), F32), jnp.zeros((8, wide), F32)]
-            for k in range(4):
+            for k in parts:
                 at = k * 4 * half
                 weight = jnp.exp2((s_ref[g, 0, at:at + 4 * half, :] - new[1]) * FACTOR)
                 totals[1] = totals[1] + sums(weight)
@@ -231,7 +264,7 @@
                     ((y, c), (y, 1 - c), (1 - y, c), (1 - y, 1 - c))
                 ):
                     src = ident(place(step, k), yy, cc)
-                    early = jnp.minimum(span_ref[src, 0], span_ref[src, 1]) < own_low
+                    early = jnp.minimum(span_ref[0, src], span_ref[1, src]) < own_low
                     spot = at + j * half
                     peak = jnp.where(early, new[0], new[1])
                     weight = jnp.exp2((s_ref[g, 1, spot:spot + half, :] - peak) * FACTOR)
@@ -239,10 +272,14 @@
                     totals[0] = totals[0] + jnp.where(early, part, 0.0)
                     totals[1] = totals[1] + jnp.where(early, 0.0, part)
                     pb_ref[spot:spot + half, :] = weight.astype(BF16)
-            mixed = jnp.dot(vtb_ref[g], pb_ref[...], preferred_element_type=F32)
+            mixed = jnp.dot(
+                vtb_ref[g, :, span], pb_ref[span, :], preferred_element_type=F32
+            )
             added = [
                 mixed[:HEAD],
-                mixed[HEAD:] + jnp.dot(vta_ref[g], pa_ref[...], preferred_element_type=F32),
+                mixed[HEAD:] + jnp.dot(
+                    vta_ref[g, :, span], pa_ref[span, :], preferred_element_type=F32
+                ),
             ]
             if first:
                 weight = jnp.exp2((s_ref[g, 1, 16 * half:17 * half, :] - new[0]) * FACTOR)
@@ -264,38 +301,74 @@
     def nothing():
         return [[jnp.full((8, wide), LOW, F32) for t in range(2)] for g in range(kv_heads)]
 
+    everything = range(4)
     peaks = nothing()
-    arrived(c_peer)
-    pass_on(0, 0)
-    take(0, 1)
-    arrived(ident(z, 1 - y, 1 - c))
-    score(z, 0, True, peaks)
-    take(0, 2)
-    pass_on(0, 1)
-    take(0, 3)
-    last(0, 1)
-    score(place(0, 1), 1, False, peaks)
-    pass_on(0, 2)
-    last(0, 2)
-    score(place(0, 2), 2, False, peaks)
-    pass_on(0, 3)
-    last(0, 3)
-    score(place(0, 3), 3, False, peaks)
-    absorb(0, True, peaks)
-
-    def further(step, carry):
+    if lanes_z == 4:
+        z1, z2, z3 = (place(0, k) for k in range(1, 4))
+        for i in range(chunks // 2):
+            query(i)
+        forward(1, 0)
+        pass_on(z, 0)
+        for i in range(chunks // 2, chunks - 1):
+            query(i)
+        forward(1, 1)
+        pass_on(z, 1)
+        query(chunks - 1)
+        forward(2, 0)
+        pass_on(z1, 0)
+        last(z)
+        score(z, 0, True, peaks)
+        forward(2, 1)
+        pass_on(z1, 1)
+        last(z1)
+        score(z1, 1, False, peaks)
+        forward(3, 0)
+        pass_on(z2, 0)
+        absorb(0, 0, (0, 1), True, peaks)
+        forward(3, 1)
+        pass_on(z2, 1)
+        for g in range(1, kv_heads):
+            absorb(g, 0, (0, 1), True, peaks)
+        pass_on(z3, 0)
         peaks = nothing()
-        for k in range(4):
-            take(step, k)
-        for k in range(4):
-            pass_on(step, k)
-        for k in range(4):
-            last(step, k)
-            score(place(step, k), k, False, peaks)
-        absorb(step, False, peaks)
-        return carry
-
-    if lanes_z > 4:
+        last(z2)
+        score(z2, 2, False, peaks)
+        pass_on(z3, 1)
+        last(z3)
+        score(z3, 3, False, peaks)
+        for g in range(kv_heads):
+            absorb(g, 0, (2, 3), False, peaks)
+    else:
+        for i in range(chunks):
+            query(i)
+        for p in range(2):
+            pass_on(z, p)
+
+        def relay(t, carry):
+            for p in range(2):
+                forward(t, p)
+                pl.when(z >= t)(lambda: pass_on(z - t, p))
+                pl.when(z + t < lanes_z)(lambda: pass_on(z + t, p))
+            return carry
+
+        lax.fori_loop(1, lanes_z, relay, 0)
+        last(z)
+        score(z, 0, True, peaks)
+        for k in range(1, 4):
+            last(place(0, k))
+            score(place(0, k), k, False, peaks)
+        for g in range(kv_heads):
+            absorb(g, 0, everything, True, peaks)
+
+        def further(step, carry):
+            peaks = nothing()
+            for k in everything:
+                last(place(step, k))
+                score(place(step, k), k, False, peaks)
+            for g in range(kv_heads):
+                absorb(g, step, everything, False, peaks)
+            return carry
+
         lax.fori_loop(1, lanes_z // 4, further, 0)
 
     for g in range(kv_heads):
@@ -311,12 +384,16 @@
                 out_ref[:half, at:at + HEAD] = first[e * half:(e + 1) * half]
                 out_ref[half:, at:at + HEAD] = second[e * half:(e + 1) * half]
 
-    for i in range(len(others)):
-        send(me, y_peer, z_sem.at[i]).wait_send()
-    for i in range(lanes_z):
-        send(me, y_peer, y_sem.at[i]).wait_send()
-    for i in range(2 * lanes_z):
-        send(me, y_peer, c_sem.at[i]).wait_send()
+    def drain(zz, carry):
+        for p in range(2):
+            to_y(zz, p).wait_send()
+            to_core(zz, 0, p).wait_send()
+            to_core(zz, 1, p).wait_send()
+            pl.when(jnp.logical_and(zz <= z, above))(lambda: to_above(zz, p).wait_send())
+            pl.when(jnp.logical_and(zz >= z, below))(lambda: to_below(zz, p).wait_send())
+        return carry
+
+    lax.fori_loop(0, lanes_z, drain, 0)
 
 
 def solution(mesh):
@@ -337,11 +414,12 @@
             functools.partial(kernel, n, heads, kv_heads),
             out_shape=jax.ShapeDtypeStruct((rows, heads * HEAD), BF16),
             in_specs=[
-                vmem, pl.BlockSpec(memory_space=pltpu.SMEM), vmem,
+                anywhere, pl.BlockSpec(memory_space=pltpu.SMEM), vmem,
                 anywhere, anywhere, anywhere, vmem, vmem, vmem,
             ],
             out_specs=vmem,
             scratch_shapes=[
+                pltpu.VMEM((rows, depth), BF16),
                 pltpu.VMEM((chunks, depth, chunk), BF16),
                 pltpu.VMEM((depth, kv_heads * HEAD), BF16),
                 pltpu.VMEM((depth, kv_heads * HEAD), BF16),
@@ -356,17 +434,18 @@
                 pltpu.VMEM((kv_heads, 2, HEAD, wide), F32),
                 pltpu.VMEM((kv_heads, 2, 1, wide), F32),
                 pltpu.VMEM((kv_heads, 2, 1, wide), F32),
-                pltpu.SemaphoreType.DMA((2 + chunks,)),
-                pltpu.SemaphoreType.DMA((n,)),
-                pltpu.SemaphoreType.DMA((n // 4,)),
-                pltpu.SemaphoreType.DMA((n // 4,)),
-                pltpu.SemaphoreType.DMA((n // 2,)),
+                pltpu.SemaphoreType.DMA((3 + chunks,)),
+                pltpu.SemaphoreType.DMA((n, 2)),
+                pltpu.SemaphoreType.DMA((n // 4, 2)),
+                pltpu.SemaphoreType.DMA((n // 4, 2)),
+                pltpu.SemaphoreType.DMA((n // 4, 2)),
+                pltpu.SemaphoreType.DMA((n // 2, 2)),
             ],
             compiler_params=pltpu.CompilerParams(
                 collective_id=0, has_side_effects=True, vmem_limit_bytes=60 * 1024 * 1024
             ),
         )(
-            hidden_in, span_order, norm_gain.reshape(1, -1), w_query, w_key, w_value,
+            hidden_in, span_order.T, norm_gain.reshape(1, -1), w_query, w_key, w_value,
             query_gain.reshape(1, -1), key_gain.reshape(1, -1), inverse,
         )
 

time: 30.8 us -> 27.2 us (0.88)
  Pallas kernels: 27.4 us -> 25.1 us
  local copies, waits for them, and re-layouts: 3.23 us -> 1.88 us
    pallas_call x1, Pallas kernels: 27.4 us -> 25.1 us  [body(): pl.pallas_call(functools.partial(kernel, n, heads, kv_heads), out_shape=j...]
    unnamed x2 -> x1, local copies, waits for them, and re-layouts: 3.23 us -> 1.88 us
where the time goes in v2:
time: 27.2 us; the launch traced here: 27 us
  Pallas kernels  25.1 us (92%)
  local copies, waits for them, and re-layouts  1.88 us (7%)
    pallas_call x1, Pallas kernels, body(): pl.pallas_call(functools.partial(kernel, n, heads, kv_heads), out_shape=j...  25.1 us
    unnamed x1, local copies, waits for them, and re-layouts  1.88 us

profile of v2, /device:TPU:1, one launch (start us, length us, event | category | flops | bytes accessed | tf_op | source)
XLA Modules:
  0.0 27.0 jit_solution(14116730037574254990)
XLA Ops:
  0.0 25.1 %shard_map.91 = bf16[128,2048]{1,0:T(8,128)(2,1)} custom-call(bf16[128,2048]{1,0:T(8,128)(2,1)} %hidden_hbm.1, s32[2,16]{1,0:T(2,128)} %bitcast.5, f32[1,2048]{1,0:T(1,128)} %bitcast.4, bf16[2048,2048]{1,0:T(8,128)(2,1)} %wq_hbm.1, bf16[2048,256]{1,0:T(8,128)(2,1)} %wk_hbm.1, bf16[2048,256]{1,0:T(8,128)(2,1)} %wv_hbm.1, f32[1,128]{1,0:T(1,128)} %bitcast.6, ...), custom_call_target="tpu_custom_call" | custom-call | tf_op jit(solution)/shard_map/pallas_call | solution.py:413
  25.1 1.9 %copy.11 = bf16[128,2048]{1,0:T(8,128)(2,1)} copy(bf16[128,2048]{1,0:T(8,128)(2,1)} %shard_map.91) | data formatting | bytes 1048576
